TPU v7x, 32 devices: a whole 2x2x4 slice. The times are simulated.
32 devices in a mesh: section: 4 (over x, core), tp: 8 (over z, y).
Axes of the slice: x: 2, y: 2, z: 4, core: 2. Of those that a mesh axis runs over, the one named last changes fastest.
Arguments:
- pending_activation: bfloat16 [4, 128, 4096], P('section'), may hold values from -6 to 6
- admissible_microbatches: bfloat16 [4, 128, 4096], P(None, None, 'tp'), may hold values from -6 to 6
- arrival_plan: int32 [4], replicated, may hold values from 0 to 3, each once
- vanished_hop: int32 [1], replicated, may hold values from 1 to 3
- query_key_value_matrices: bfloat16 [4, 4096, 3, 2048], P('section', None, None, 'tp')
- mixing_projection_matrices: bfloat16 [4, 2048, 4096], P('section', 'tp'), may hold values from -0.125 to 0.125
- normalizer_factors: bfloat16 [4, 4096], P('section'), may hold values from 0.25 to 1.75
Outputs:
- activation_later: bfloat16 [4, 128, 4096], P('section')
- standby_input: bfloat16 [4, 128, 4096], P('section', None, 'tp')
Inputs may be any that keep to these rules, and one draw needn't show every extreme that they name: `vanished_hop`: the preempted section is not the first. `arrival_plan`: each micro-batch index once.
All inputs are finite; a program needn't handle non-finite values.
Results may differ from a plain program's by a relative error of at most 0.013.
Values may be sent and summed in bfloat16 or wider, within the bound.
A program may use at most 64 MiB of HBM per device.

v0:
```python
import jax
import jax.numpy as jnp
from jax import lax
from jax.sharding import PartitionSpec as P

HD = 128
TICKS = 3
NORM_EPS = 1e-05


def shifted(value, axis, steps):
    count = lax.axis_size(axis)
    pairs = [(source, (source + steps) % count) for source in range(count)]
    return lax.ppermute(value, axis, pairs)


def layer_norm(x_rows, scale_row):
    widened = x_rows.astype(jnp.float32)
    row_mean = jnp.mean(widened, axis=-1, keepdims=True)
    centered = widened - row_mean
    row_var = jnp.mean(centered * centered, axis=-1, keepdims=True)
    return (centered * lax.rsqrt(row_var + NORM_EPS) * scale_row.astype(jnp.float32)).astype(
        jnp.bfloat16
    )


def attend(normed, w_in, w_out):
    row_count = normed.shape[0]
    col_count = w_in.shape[2]
    head_count = col_count // HD
    projected = jnp.dot(
        normed, w_in.reshape(w_in.shape[0], 3 * col_count), preferred_element_type=jnp.float32
    )
    projected = projected.astype(jnp.bfloat16).reshape(row_count, 3, head_count, HD)
    queries = projected[:, 0]
    key_rows = projected[:, 1]
    values = projected[:, 2]
    scores = jnp.einsum(
        "qhd,khd->hqk", queries, key_rows, preferred_element_type=jnp.float32
    ) * HD ** (-0.5)
    causal = jnp.arange(row_count)[:, None] >= jnp.arange(row_count)[None, :]
    scores = jnp.where(causal[None], scores, -jnp.inf)
    row_max = jnp.max(scores, axis=-1, keepdims=True)
    weights = jnp.exp(scores - row_max)
    probs = (weights / jnp.sum(weights, axis=-1, keepdims=True)).astype(jnp.bfloat16)
    context = jnp.einsum("hqk,khd->qhd", probs, values, preferred_element_type=jnp.float32)
    context = context.astype(jnp.bfloat16).reshape(row_count, col_count)
    return jnp.dot(context, w_out, preferred_element_type=jnp.float32)


def per_device(
    pending_activation,
    admissible_microbatches,
    arrival_plan,
    vanished_hop,
    query_key_value_matrices,
    mixing_projection_matrices,
    normalizer_factors,
):
    sections = lax.axis_size("section")
    my_section = lax.axis_index("section")
    sharding_degree = lax.axis_size("tp")
    slice_breadth = pending_activation.shape[2] // sharding_degree
    col_start = lax.axis_index("tp") * slice_breadth
    lost_at = vanished_hop[0]
    is_pred = my_section == lost_at - 1
    is_next = my_section == lost_at + 1
    is_lost = my_section == lost_at
    w_in = query_key_value_matrices[0]
    w_out = mixing_projection_matrices[0]
    scale_row = normalizer_factors[0]
    entire_source_lines = pending_activation[0]
    x_sh = lax.dynamic_slice_in_dim(entire_source_lines, col_start, slice_breadth, 1)
    blank = jnp.zeros(entire_source_lines.shape, jnp.float32)
    far_in, far_out, far_gain = shifted((w_in, w_out, scale_row), "section", -1)

    def successor_layer(rows_full):
        return attend(layer_norm(rows_full, far_gain), far_in, far_out)

    standby_sh = x_sh
    for tick_index in range(TICKS):
        own_part = attend(layer_norm(entire_source_lines, scale_row), w_in, w_out)
        ya_sh = (
            x_sh.astype(jnp.float32)
            + lax.psum_scatter(own_part, "tp", scatter_dimension=1, tiled=True)
        ).astype(jnp.bfloat16)
        ya_full = lax.all_gather(ya_sh, "tp", axis=1, tiled=True)
        spare_part = (
            successor_layer(ya_full)
            if tick_index == TICKS - 1
            else lax.cond(is_pred, lambda: successor_layer(ya_full), lambda: blank)
        )
        spare_sh = (
            ya_sh.astype(jnp.float32)
            + lax.psum_scatter(spare_part, "tp", scatter_dimension=1, tiled=True)
        ).astype(jnp.bfloat16)
        result_sh = jnp.where(is_pred, spare_sh, ya_sh)
        entering = lax.dynamic_index_in_dim(
            admissible_microbatches, arrival_plan[tick_index], 0, keepdims=False
        )
        send_sh = jnp.where(my_section == sections - 1, entering, result_sh)
        near_rows = shifted(send_sh, "section", 1)
        far_rows = shifted(spare_sh, "section", 2)
        x_sh = jnp.where(is_lost, jnp.zeros_like(far_rows), jnp.where(is_next, far_rows, near_rows))
        entire_source_lines = lax.all_gather(x_sh, "tp", axis=1, tiled=True)
        standby_sh = far_rows
    return (entire_source_lines[None], standby_sh[None])


def solution(mesh):
    placed = (
        P("section", None, None),
        P(None, None, "tp"),
        P(),
        P(),
        P("section", None, None, "tp"),
        P("section", "tp", None),
        P("section", None),
    )
    return jax.shard_map(
        per_device,
        mesh=mesh,
        in_specs=placed,
        out_specs=(P("section", None, None), P("section", None, "tp")),
        check_vma=False,
    )
```

profile of v0, /device:TPU:0, one launch (start us, length us, event | category | flops | bytes accessed | tf_op | source)
XLA Modules:
  0.0 769.3 jit_solution(308551706380850222)
XLA Ops:
  7.2 8.8 %copy.42 = bf16[1,4096,3,256]{1,3,2,0:T(8,128)(2,1)} copy(bf16[1,4096,3,256]{3,1,2,0:T(8,128)(2,1)} %param.15) | data formatting | bytes 12582912 | tf_op args[4]
  19.9 5.2 convolution_convert_fusion.7
  29.1 68.7 %reduce-scatter.7.cloned.1.call-done = f32[128,512]{1,0:T(8,128)} async-done(((f32[128,4096]{1,0:T(8,128)}), f32[128,512]{1,0:T(8,128)}) %reduce-scatter.7.cloned.1.call-update) | async-done | bytes 262160 | tf_op jit(solution)/shard_map/reduce_scatter | solution.py:85
  100.3 9.4 %collective-permute-done = bf16[4096]{0:T(1024)(128)(2,1)S(1)} collective-permute-done((bf16[4096]{0:T(1024)(128)(2,1)S(1)}, bf16[4096]{0:T(1024)(128)(2,1)S(1)}, u32[]{:S(2)}, u32[]{:S(2)}) %collective-permute-start) | collective-permute-done | bytes 8224 | tf_op jit(solution)/shard_map/ppermute | solution.py:14
  109.7 29.2 %all-gather.7.cloned.1.call-done = bf16[128,4096]{1,0:T(8,128)(2,1)} async-done(((bf16[128,512]{1,0:T(8,128)(2,1)}), bf16[128,4096]{1,0:T(8,128)(2,1)}) %all-gather.7.cloned.1.call-update) | async-done | bytes 1048592 | tf_op jit(solution)/shard_map/all_gather | solution.py:87
  138.9 12.4 %conditional.2 = (f32[128,4096]{1,0:T(8,128)}) conditional(s32[]{:T(128)} %convert_element_type.183, () %tuple.20, (bf16[128,4096]{1,0:T(8,128)(2,1)}, bf16[4096]{0:T(1024)(128)(2,1)S(1)}, bf16[4096,3,256]{0,2,1:T(8,128)(2,1)}, bf16[256,4096]{1,0:T(8,128)(2,1)}) %tuple.21), branch_computations={%region_5.6_spmd, %region_6.11_spmd} | conditional | flops 1096667776 | bytes 19741220 | solution.py:91
  142.2 5.0 convolution_convert_fusion
  154.6 64.0 %reduce-scatter.9.cloned.1.call-done = f32[128,512]{1,0:T(8,128)} async-done(((f32[128,4096]{1,0:T(8,128)}), f32[128,512]{1,0:T(8,128)}) %reduce-scatter.9.cloned.1.call-update) | async-done | bytes 262160 | tf_op jit(solution)/shard_map/reduce_scatter | solution.py:95
  221.2 4.0 collective-permute-done.3
  226.8 38.5 %all-gather.9.cloned.1.call-done = bf16[128,4096]{1,0:T(8,128)(2,1)} async-done(((bf16[128,512]{1,0:T(8,128)(2,1)}), bf16[128,4096]{1,0:T(8,128)(2,1)}) %all-gather.9.cloned.1.call-update) | async-done | bytes 1048592 | tf_op jit(solution)/shard_map/all_gather | solution.py:105
  268.6 5.0 convolution_convert_fusion.6
  276.2 68.0 %reduce-scatter.11.cloned.1.call-done = f32[128,512]{1,0:T(8,128)} async-done(((f32[128,4096]{1,0:T(8,128)}), f32[128,512]{1,0:T(8,128)}) %reduce-scatter.11.cloned.1.call-update) | async-done | bytes 262160 | tf_op jit(solution)/shard_map/reduce_scatter | solution.py:85
  346.0 39.2 %all-gather.11.cloned.1.call-done = bf16[128,4096]{1,0:T(8,128)(2,1)} async-done(((bf16[128,512]{1,0:T(8,128)(2,1)}), bf16[128,4096]{1,0:T(8,128)(2,1)}) %all-gather.11.cloned.1.call-update) | async-done | bytes 1048592 | tf_op jit(solution)/shard_map/all_gather | solution.py:87
  385.2 12.4 %conditional.3 = (f32[128,4096]{1,0:T(8,128)}) conditional(s32[]{:T(128)} %convert_element_type.183, () %tuple.22, (bf16[128,4096]{1,0:T(8,128)(2,1)}, bf16[4096]{0:T(1024)(128)(2,1)S(1)}, bf16[4096,3,256]{0,2,1:T(8,128)(2,1)}, bf16[256,4096]{1,0:T(8,128)(2,1)}) %tuple.23), branch_computations={%region_17.18_spmd, %region_18.23_spmd} | conditional | flops 1096667776 | bytes 19741220 | solution.py:91
  388.4 5.0 convolution_convert_fusion.2
  399.6 65.4 %reduce-scatter.13.cloned.1.call-done = f32[128,512]{1,0:T(8,128)} async-done(((f32[128,4096]{1,0:T(8,128)}), f32[128,512]{1,0:T(8,128)}) %reduce-scatter.13.cloned.1.call-update) | async-done | bytes 262160 | tf_op jit(solution)/shard_map/reduce_scatter | solution.py:95
  473.3 38.5 %all-gather.13.cloned.1.call-done = bf16[128,4096]{1,0:T(8,128)(2,1)} async-done(((bf16[128,512]{1,0:T(8,128)(2,1)}), bf16[128,4096]{1,0:T(8,128)(2,1)}) %all-gather.13.cloned.1.call-update) | async-done | bytes 1048592 | tf_op jit(solution)/shard_map/all_gather | solution.py:105
  515.0 5.0 convolution_convert_fusion.5
  522.7 68.3 %reduce-scatter.15.cloned.1.call-done = f32[128,512]{1,0:T(8,128)} async-done(((f32[128,4096]{1,0:T(8,128)}), f32[128,512]{1,0:T(8,128)}) %reduce-scatter.15.cloned.1.call-update) | async-done | bytes 262160 | tf_op jit(solution)/shard_map/reduce_scatter | solution.py:85
  592.7 39.2 %all-gather.15.cloned.1.call-done = bf16[128,4096]{1,0:T(8,128)(2,1)} async-done(((bf16[128,512]{1,0:T(8,128)(2,1)}), bf16[128,4096]{1,0:T(8,128)(2,1)}) %all-gather.15.cloned.1.call-update) | async-done | bytes 1048592 | tf_op jit(solution)/shard_map/all_gather | solution.py:87
  635.2 5.0 convolution_convert_fusion.4
  646.5 66.3 %reduce-scatter.17.cloned.1.call-done = f32[128,512]{1,0:T(8,128)} async-done(((f32[128,4096]{1,0:T(8,128)}), f32[128,512]{1,0:T(8,128)}) %reduce-scatter.17.cloned.1.call-update) | async-done | bytes 262160 | tf_op jit(solution)/shard_map/reduce_scatter | solution.py:95
  715.3 4.1 collective-permute-done.7
  720.9 38.5 %all-gather.17.cloned.1.call-done = bf16[128,4096]{1,0:T(8,128)(2,1)} async-done(((bf16[128,512]{1,0:T(8,128)(2,1)}), bf16[128,4096]{1,0:T(8,128)(2,1)}) %all-gather.17.cloned.1.call-update) | async-done | bytes 1048592 | tf_op jit(solution)/shard_map/all_gather | solution.py:105
  (161 shorter events, 67.6 us)
Async XLA Ops:
  7.2 90.7 %reduce-scatter.7.cloned.1.call-start = ((), (), s32[]{:S(2)}) async-start(), calls=%async_computation.6 | async-start | bytes 2359296 | tf_op jit(solution)/shard_map/reduce_scatter | solution.py:85
  16.1 122.9 %collective-permute-start.1 = (bf16[4096,3,256]{0,2,1:T(8,128)(2,1)}, bf16[4096,3,256]{0,2,1:T(8,128)(2,1)}, u32[]{:S(2)}, u32[]{:S(2)}) collective-permute-start(bf16[4096,3,256]{0,2,1:T(8,128)(2,1)} %bitcast.141), channel_id=1, source_target_pairs={{0,24},{8,0},{16,8},{24,16},{1,25},{9,1},{17,9},{25,17},{2,26},{10... | collective-permute-start | bytes 18874376 | tf_op jit(solution)/shard_map/ppermute | solution.py:14
  28.3 110.6 %all-gather.7.cloned.1.call-start = ((), (), s32[]{:S(2)}) async-start(), calls=%async_computation.7 | async-start | bytes 1179648 | tf_op jit(solution)/shard_map/all_gather | solution.py:87
  28.4 81.3 %collective-permute-start.2 = (bf16[256,4096]{1,0:T(8,128)(2,1)S(1)}, bf16[256,4096]{1,0:T(8,128)(2,1)}, u32[]{:S(2)}, u32[]{:S(2)}) collective-permute-start(bf16[256,4096]{1,0:T(8,128)(2,1)S(1)} %bitcast.140), channel_id=1, source_target_pairs={{0,24},{8,0},{16,8},{24,16},{1,25},{9,1},{17,9},{25,17},{2,26},{10... | collective-permute-start | bytes 6291464 | tf_op jit(solution)/shard_map/ppermute | solution.py:14
  99.5 119.0 %reduce-scatter.9.cloned.1.call-start = ((), (), s32[]{:S(2)}) async-start(), calls=%async_computation.8 | async-start | bytes 2359296 | tf_op jit(solution)/shard_map/reduce_scatter | solution.py:95
  99.6 10.2 %collective-permute-start = (bf16[4096]{0:T(1024)(128)(2,1)S(1)}, bf16[4096]{0:T(1024)(128)(2,1)S(1)}, u32[]{:S(2)}, u32[]{:S(2)}) collective-permute-start(bf16[4096]{0:T(1024)(128)(2,1)S(1)} %reduce.1), channel_id=1, source_target_pairs={{0,24},{8,0},{16,8},{24,16},{1,25},{9,1},{17,9},{25,17},{2,26},{10... | collective-permute-start | bytes 24584 | tf_op jit(solution)/shard_map/ppermute | solution.py:14
  151.4 117.1 %copy-start.14 = (f32[4096]{0:T(1024)S(1)}, f32[4096]{0:T(1024)}, u32[]{:S(2)}) copy-start(f32[4096]{0:T(1024)} %copy-done.13) | copy-start | bytes 49156
  151.4 113.9 %all-gather.9.cloned.1.call-start = ((), (), s32[]{:S(2)}) async-start(), calls=%async_computation.9 | async-start | bytes 1179648 | tf_op jit(solution)/shard_map/all_gather | solution.py:105
  219.6 5.5 collective-permute-start.3
  221.2 4.9 collective-permute-start.4
  226.8 117.5 %reduce-scatter.11.cloned.1.call-start = ((), (), s32[]{:S(2)}) async-start(), calls=%async_computation.10 | async-start | bytes 2359296 | tf_op jit(solution)/shard_map/reduce_scatter | solution.py:85
  276.2 109.0 %all-gather.11.cloned.1.call-start = ((), (), s32[]{:S(2)}) async-start(), calls=%async_computation.11 | async-start | bytes 1179648 | tf_op jit(solution)/shard_map/all_gather | solution.py:87
  345.9 119.2 %reduce-scatter.13.cloned.1.call-start = ((), (), s32[]{:S(2)}) async-start(), calls=%async_computation.12 | async-start | bytes 2359296 | tf_op jit(solution)/shard_map/reduce_scatter | solution.py:95
  397.6 114.2 %all-gather.13.cloned.1.call-start = ((), (), s32[]{:S(2)}) async-start(), calls=%async_computation.13 | async-start | bytes 1179648 | tf_op jit(solution)/shard_map/all_gather | solution.py:105
  466.1 5.5 collective-permute-start.5
  467.6 4.9 collective-permute-start.6
  473.2 117.7 %reduce-scatter.15.cloned.1.call-start = ((), (), s32[]{:S(2)}) async-start(), calls=%async_computation.14 | async-start | bytes 2359296 | tf_op jit(solution)/shard_map/reduce_scatter | solution.py:85
  522.6 68.4 %copy-start.8 = (bf16[128,512]{1,0:T(8,128)(2,1)S(1)}, bf16[128,512]{1,0:T(8,128)(2,1)}, u32[]{:S(2)}) copy-start(bf16[128,512]{1,0:T(8,128)(2,1)} %select_select_fusion.1) | copy-start | bytes 393220
  522.6 109.3 %all-gather.15.cloned.1.call-start = ((), (), s32[]{:S(2)}) async-start(), calls=%async_computation.15 | async-start | bytes 1179648 | tf_op jit(solution)/shard_map/all_gather | solution.py:87
  592.6 120.1 %reduce-scatter.17.cloned.1.call-start = ((), (), s32[]{:S(2)}) async-start(), calls=%async_computation.16 | async-start | bytes 2359296 | tf_op jit(solution)/shard_map/reduce_scatter | solution.py:95
  644.4 68.4 %copy-start.11 = (bf16[128,512]{1,0:T(8,128)(2,1)S(1)}, bf16[128,512]{1,0:T(8,128)(2,1)}, u32[]{:S(2)}) copy-start(bf16[128,512]{1,0:T(8,128)(2,1)} %add_convert_fusion.1) | copy-start | bytes 393220
  644.4 115.1 %all-gather.17.cloned.1.call-start = ((), (), s32[]{:S(2)}) async-start(), calls=%async_computation.17 | async-start | bytes 1179648 | tf_op jit(solution)/shard_map/all_gather | solution.py:105
  713.8 5.6 collective-permute-start.7
  715.3 4.9 collective-permute-start.8
  (15 other events, 323.5 us)
Sparse Core Ops, SparseCore 0:
  28.5 69.3 reduce-scatter.6
  100.5 38.4 all-gather.6
  151.5 66.9 reduce-scatter.8
  226.9 38.3 all-gather.8
  276.3 67.8 reduce-scatter.10
  346.7 38.3 all-gather.10
  397.7 67.2 reduce-scatter.12
  473.4 38.3 all-gather.12
  522.8 68.1 reduce-scatter.14
  593.4 38.4 all-gather.14
  644.5 68.2 reduce-scatter.16
  721.0 38.3 all-gather.16
where the time goes:
time: 771 us; the launch traced here: 769 us
  waiting for transfers between devices  648 us (84%)
  matrix products  48.7 us (6%)
  other arithmetic  27.9 us (4%)
  between operations  21.1 us (3%)
  local copies, waits for them, and re-layouts  14.9 us (2%)
  starting transfers between devices  8.26 us (1%)
    reduce_scatter x3, waiting for transfers between devices, per_device(): lax.psum_scatter(own_part, 'tp', scatter_dimension=1, tiled=True)  205 us
    reduce_scatter x3, waiting for transfers between devices, per_device(): lax.psum_scatter(spare_part, 'tp', scatter_dimension=1, tiled=True)  196 us
    all_gather x3, waiting for transfers between devices, per_device(): entire_source_lines = lax.all_gather(x_sh, 'tp', axis=1, tiled=True)  116 us
    all_gather x3, waiting for transfers between devices, per_device(): ya_full = lax.all_gather(ya_sh, 'tp', axis=1, tiled=True)  108 us
    dot_general x6, matrix products, attend(): jnp.dot(normed, w_in.reshape(w_in.shape[0], 3 * col_count), preferred_ele...  30.3 us
    ppermute x9, waiting for transfers between devices, shifted(): return lax.ppermute(value, axis, pairs)  24.2 us
    dot_general x6, matrix products, attend(): return jnp.dot(context, w_out, preferred_element_type=jnp.float32)  15.6 us
  transfers between devices with their start and end apart: 21, of which 19 were waited for; matrix products, arithmetic and copies ran while one was open for 2% of the time, Pallas kernels for 0%

commit v1 on v0

--- a/solution.py
+++ b/solution.py
@@ -102,7 +102,14 @@
         near_rows = shifted(send_sh, "section", 1)
         far_rows = shifted(spare_sh, "section", 2)
         x_sh = jnp.where(is_lost, jnp.zeros_like(far_rows), jnp.where(is_next, far_rows, near_rows))
-        entire_source_lines = lax.all_gather(x_sh, "tp", axis=1, tiled=True)
+        ring = [x_sh]
+        for hop in range(7):
+            ring.append(lax.ppermute(ring[-1], "tp", [(dev, (dev + 1) % 8) for dev in range(8)]))
+        entire_source_lines = jnp.roll(
+            jnp.concatenate(ring[::-1], axis=1),
+            (lax.axis_index("tp") + 1) * ring[0].shape[1],
+            axis=1,
+        )
         standby_sh = far_rows
     return (entire_source_lines[None], standby_sh[None])
 

time: 771 us -> 810 us (1.051)
  waiting for transfers between devices: 648 us -> 693 us
    ppermute x0 -> x21, waiting for transfers between devices: none -> 166 us  [per_device(): lax.ppermute(ring[-1], 'tp', [(dev, (dev + 1) % 8) for dev in range(8)])]
    all_gather x3 -> x0, waiting for transfers between devices: 116 us -> none  [per_device(): entire_source_lines = lax.all_gather(x_sh, 'tp', axis=1, tiled=True)]
  transfers between devices with their start and end apart: 21 -> 39, of which waited for: 19 -> 37; matrix products, arithmetic and copies ran while one was open for 2% -> 1% of each run, Pallas kernels for 0% -> 0%
where the time goes in v1:
time: 810 us; the launch traced here: 809 us
  waiting for transfers between devices  693 us (86%)
  matrix products  48.7 us (6%)
  other arithmetic  23.2 us (3%)
  between operations  21 us (3%)
  local copies, waits for them, and re-layouts  12.9 us (2%)
  starting transfers between devices  10.2 us (1%)
    reduce_scatter x3, waiting for transfers between devices, per_device(): lax.psum_scatter(own_part, 'tp', scatter_dimension=1, tiled=True)  200 us
    reduce_scatter x3, waiting for transfers between devices, per_device(): lax.psum_scatter(spare_part, 'tp', scatter_dimension=1, tiled=True)  195 us
    ppermute x21, waiting for transfers between devices, per_device(): lax.ppermute(ring[-1], 'tp', [(dev, (dev + 1) % 8) for dev in range(8)])  166 us
    all_gather x3, waiting for transfers between devices, per_device(): ya_full = lax.all_gather(ya_sh, 'tp', axis=1, tiled=True)  108 us
    dot_general x6, matrix products, attend(): jnp.dot(normed, w_in.reshape(w_in.shape[0], 3 * col_count), preferred_ele...  30.3 us
    ppermute x9, waiting for transfers between devices, shifted(): return lax.ppermute(value, axis, pairs)  24.1 us
  transfers between devices with their start and end apart: 39, of which 37 were waited for; matrix products, arithmetic and copies ran while one was open for 1% of the time, Pallas kernels for 0%

profile of v1, /device:TPU:0, one launch (start us, length us, event | category | flops | bytes accessed | tf_op | source)
XLA Modules:
  0.0 809.0 jit_solution(16168596121461015605)
XLA Ops:
  7.2 8.8 %copy.42 = bf16[1,4096,3,256]{1,3,2,0:T(8,128)(2,1)} copy(bf16[1,4096,3,256]{3,1,2,0:T(8,128)(2,1)} %param.17) | data formatting | bytes 12582912 | tf_op args[4]
  29.1 68.7 %reduce-scatter.7.cloned.1.call-done = f32[128,512]{1,0:T(8,128)} async-done(((f32[128,4096]{1,0:T(8,128)}), f32[128,512]{1,0:T(8,128)}) %reduce-scatter.7.cloned.1.call-update) | async-done | bytes 262160 | tf_op jit(solution)/shard_map/reduce_scatter | solution.py:85
  100.3 9.4 %collective-permute-done = bf16[4096]{0:T(1024)(128)(2,1)S(1)} collective-permute-done((bf16[4096]{0:T(1024)(128)(2,1)S(1)}, bf16[4096]{0:T(1024)(128)(2,1)S(1)}, u32[]{:S(2)}, u32[]{:S(2)}) %collective-permute-start) | collective-permute-done | bytes 8224 | tf_op jit(solution)/shard_map/ppermute | solution.py:14
  109.7 29.2 %all-gather.4.cloned.1.call-done = bf16[128,4096]{1,0:T(8,128)(2,1)} async-done(((bf16[128,512]{1,0:T(8,128)(2,1)}), bf16[128,4096]{1,0:T(8,128)(2,1)}) %all-gather.4.cloned.1.call-update) | async-done | bytes 1048592 | tf_op jit(solution)/shard_map/all_gather | solution.py:87
  138.9 12.4 %conditional.2 = (f32[128,4096]{1,0:T(8,128)}) conditional(s32[]{:T(128)} %convert_element_type.183, () %tuple.21, (bf16[128,4096]{1,0:T(8,128)(2,1)}, bf16[4096]{0:T(1024)(128)(2,1)S(1)}, bf16[4096,3,256]{0,2,1:T(8,128)(2,1)}, bf16[256,4096]{1,0:T(8,128)(2,1)}) %tuple.22), branch_computations={%region_5.6_spmd, %region_6.11_spmd} | conditional | flops 1096667776 | bytes 19741220 | solution.py:91
  154.6 64.0 %reduce-scatter.9.cloned.1.call-done = f32[128,512]{1,0:T(8,128)} async-done(((f32[128,4096]{1,0:T(8,128)}), f32[128,512]{1,0:T(8,128)}) %reduce-scatter.9.cloned.1.call-update) | async-done | bytes 262160 | tf_op jit(solution)/shard_map/reduce_scatter | solution.py:95
  233.8 7.7 collective-permute-done.6
  241.5 7.7 collective-permute-done.7
  249.1 7.9 collective-permute-done.8
  257.0 9.0 %collective-permute-done.9 = bf16[128,512]{1,0:T(8,128)(2,1)S(1)} collective-permute-done((bf16[128,512]{1,0:T(8,128)(2,1)S(1)}, bf16[128,512]{1,0:T(8,128)(2,1)S(1)}, u32[]{:S(2)}, u32[]{:S(2)}) %collective-permute-start.9) | collective-permute-done | bytes 131104 | tf_op jit(solution)/shard_map/ppermute | solution.py:107
  266.1 8.2 %collective-permute-done.10 = bf16[128,512]{1,0:T(8,128)(2,1)S(1)} collective-permute-done((bf16[128,512]{1,0:T(8,128)(2,1)S(1)}, bf16[128,512]{1,0:T(8,128)(2,1)S(1)}, u32[]{:S(2)}, u32[]{:S(2)}) %collective-permute-start.10) | collective-permute-done | bytes 131104 | tf_op jit(solution)/shard_map/ppermute | solution.py:107
  291.1 65.5 %reduce-scatter.11.cloned.1.call-done = f32[128,512]{1,0:T(8,128)} async-done(((f32[128,4096]{1,0:T(8,128)}), f32[128,512]{1,0:T(8,128)}) %reduce-scatter.11.cloned.1.call-update) | async-done | bytes 262160 | tf_op jit(solution)/shard_map/reduce_scatter | solution.py:85
  358.3 39.2 %all-gather.6.cloned.1.call-done = bf16[128,4096]{1,0:T(8,128)(2,1)} async-done(((bf16[128,512]{1,0:T(8,128)(2,1)}), bf16[128,4096]{1,0:T(8,128)(2,1)}) %all-gather.6.cloned.1.call-update) | async-done | bytes 1048592 | tf_op jit(solution)/shard_map/all_gather | solution.py:87
  397.5 12.4 %conditional.3 = (f32[128,4096]{1,0:T(8,128)}) conditional(s32[]{:T(128)} %convert_element_type.183, () %tuple.23, (bf16[128,4096]{1,0:T(8,128)(2,1)}, bf16[4096]{0:T(1024)(128)(2,1)S(1)}, bf16[4096,3,256]{0,2,1:T(8,128)(2,1)}, bf16[256,4096]{1,0:T(8,128)(2,1)}) %tuple.24), branch_computations={%region_17.19_spmd, %region_18.24_spmd} | conditional | flops 1096667776 | bytes 19741220 | solution.py:91
  412.0 65.2 %reduce-scatter.13.cloned.1.call-done = f32[128,512]{1,0:T(8,128)} async-done(((f32[128,4096]{1,0:T(8,128)}), f32[128,512]{1,0:T(8,128)}) %reduce-scatter.13.cloned.1.call-update) | async-done | bytes 262160 | tf_op jit(solution)/shard_map/reduce_scatter | solution.py:95
  507.7 7.9 collective-permute-done.17
  515.6 9.0 %collective-permute-done.18 = bf16[128,512]{1,0:T(8,128)(2,1)S(1)} collective-permute-done((bf16[128,512]{1,0:T(8,128)(2,1)S(1)}, bf16[128,512]{1,0:T(8,128)(2,1)S(1)}, u32[]{:S(2)}, u32[]{:S(2)}) %collective-permute-start.18) | collective-permute-done | bytes 131104 | tf_op jit(solution)/shard_map/ppermute | solution.py:107
  524.7 8.2 %collective-permute-done.19 = bf16[128,512]{1,0:T(8,128)(2,1)S(1)} collective-permute-done((bf16[128,512]{1,0:T(8,128)(2,1)S(1)}, bf16[128,512]{1,0:T(8,128)(2,1)S(1)}, u32[]{:S(2)}, u32[]{:S(2)}) %collective-permute-start.19) | collective-permute-done | bytes 131104 | tf_op jit(solution)/shard_map/ppermute | solution.py:107
  549.5 65.7 %reduce-scatter.15.cloned.1.call-done = f32[128,512]{1,0:T(8,128)} async-done(((f32[128,4096]{1,0:T(8,128)}), f32[128,512]{1,0:T(8,128)}) %reduce-scatter.15.cloned.1.call-update) | async-done | bytes 262160 | tf_op jit(solution)/shard_map/reduce_scatter | solution.py:85
  616.9 39.4 %all-gather.8.cloned.1.call-done = bf16[128,4096]{1,0:T(8,128)(2,1)} async-done(((bf16[128,512]{1,0:T(8,128)(2,1)}), bf16[128,4096]{1,0:T(8,128)(2,1)}) %all-gather.8.cloned.1.call-update) | async-done | bytes 1048592 | tf_op jit(solution)/shard_map/all_gather | solution.py:87
  670.8 65.9 %reduce-scatter.17.cloned.1.call-done = f32[128,512]{1,0:T(8,128)} async-done(((f32[128,4096]{1,0:T(8,128)}), f32[128,512]{1,0:T(8,128)}) %reduce-scatter.17.cloned.1.call-update) | async-done | bytes 262160 | tf_op jit(solution)/shard_map/reduce_scatter | solution.py:95
  767.2 7.9 collective-permute-done.26
  775.2 9.1 %collective-permute-done.27 = bf16[128,512]{1,0:T(8,128)(2,1)S(1)} collective-permute-done((bf16[128,512]{1,0:T(8,128)(2,1)S(1)}, bf16[128,512]{1,0:T(8,128)(2,1)S(1)}, u32[]{:S(2)}, u32[]{:S(2)}) %collective-permute-start.27) | collective-permute-done | bytes 131104 | tf_op jit(solution)/shard_map/ppermute | solution.py:107
  784.2 8.2 %collective-permute-done.28 = bf16[128,512]{1,0:T(8,128)(2,1)S(1)} collective-permute-done((bf16[128,512]{1,0:T(8,128)(2,1)S(1)}, bf16[128,512]{1,0:T(8,128)(2,1)S(1)}, u32[]{:S(2)}, u32[]{:S(2)}) %collective-permute-start.28) | collective-permute-done | bytes 131104 | tf_op jit(solution)/shard_map/ppermute | solution.py:107
  (210 shorter events, 176.0 us)
Async XLA Ops:
  7.2 90.7 %reduce-scatter.7.cloned.1.call-start = ((), (), s32[]{:S(2)}) async-start(), calls=%async_computation.6 | async-start | bytes 2359296 | tf_op jit(solution)/shard_map/reduce_scatter | solution.py:85
  16.1 122.9 %collective-permute-start.1 = (bf16[4096,3,256]{0,2,1:T(8,128)(2,1)}, bf16[4096,3,256]{0,2,1:T(8,128)(2,1)}, u32[]{:S(2)}, u32[]{:S(2)}) collective-permute-start(bf16[4096,3,256]{0,2,1:T(8,128)(2,1)} %bitcast.142), channel_id=1, source_target_pairs={{0,24},{8,0},{16,8},{24,16},{1,25},{9,1},{17,9},{25,17},{2,26},{10... | collective-permute-start | bytes 18874376 | tf_op jit(solution)/shard_map/ppermute | solution.py:14
  28.3 110.6 %all-gather.4.cloned.1.call-start = ((), (), s32[]{:S(2)}) async-start(), calls=%async_computation.7 | async-start | bytes 1179648 | tf_op jit(solution)/shard_map/all_gather | solution.py:87
  28.4 81.3 %collective-permute-start.2 = (bf16[256,4096]{1,0:T(8,128)(2,1)S(1)}, bf16[256,4096]{1,0:T(8,128)(2,1)}, u32[]{:S(2)}, u32[]{:S(2)}) collective-permute-start(bf16[256,4096]{1,0:T(8,128)(2,1)S(1)} %bitcast.141), channel_id=1, source_target_pairs={{0,24},{8,0},{16,8},{24,16},{1,25},{9,1},{17,9},{25,17},{2,26},{10... | collective-permute-start | bytes 6291464 | tf_op jit(solution)/shard_map/ppermute | solution.py:14
  99.5 119.0 %reduce-scatter.9.cloned.1.call-start = ((), (), s32[]{:S(2)}) async-start(), calls=%async_computation.8 | async-start | bytes 2359296 | tf_op jit(solution)/shard_map/reduce_scatter | solution.py:95
  99.6 10.2 %collective-permute-start = (bf16[4096]{0:T(1024)(128)(2,1)S(1)}, bf16[4096]{0:T(1024)(128)(2,1)S(1)}, u32[]{:S(2)}, u32[]{:S(2)}) collective-permute-start(bf16[4096]{0:T(1024)(128)(2,1)S(1)} %reduce.1), channel_id=1, source_target_pairs={{0,24},{8,0},{16,8},{24,16},{1,25},{9,1},{17,9},{25,17},{2,26},{10... | collective-permute-start | bytes 24584 | tf_op jit(solution)/shard_map/ppermute | solution.py:14
  151.4 205.2 %reduce-scatter.11.cloned.1.call-start = ((), (), s32[]{:S(2)}) async-start(), calls=%async_computation.9 | async-start | bytes 2359296 | tf_op jit(solution)/shard_map/reduce_scatter | solution.py:85
  226.1 7.7 collective-permute-start.5
  249.1 7.9 collective-permute-start.8
  257.0 9.0 %collective-permute-start.9 = (bf16[128,512]{1,0:T(8,128)(2,1)S(1)}, bf16[128,512]{1,0:T(8,128)(2,1)S(1)}, u32[]{:S(2)}, u32[]{:S(2)}) collective-permute-start(bf16[128,512]{1,0:T(8,128)(2,1)S(1)} %collective-permute-done.8), channel_id=1, source_target_pairs={{0,1},{1,2},{2,3},{3,4},{4,5},{5,6},{6,7},{7,0},{8,9},{9,10},{10,1... | collective-permute-start | bytes 393224 | tf_op jit(solution)/shard_map/ppermute | solution.py:107
  266.1 8.2 %collective-permute-start.10 = (bf16[128,512]{1,0:T(8,128)(2,1)S(1)}, bf16[128,512]{1,0:T(8,128)(2,1)S(1)}, u32[]{:S(2)}, u32[]{:S(2)}) collective-permute-start(bf16[128,512]{1,0:T(8,128)(2,1)S(1)} %collective-permute-done.9), channel_id=1, source_target_pairs={{0,1},{1,2},{2,3},{3,4},{4,5},{5,6},{6,7},{7,0},{8,9},{9,10},{10,1... | collective-permute-start | bytes 393224 | tf_op jit(solution)/shard_map/ppermute | solution.py:107
  290.9 106.7 %all-gather.6.cloned.1.call-start = ((), (), s32[]{:S(2)}) async-start(), calls=%async_computation.10 | async-start | bytes 1179648 | tf_op jit(solution)/shard_map/all_gather | solution.py:87
  358.2 118.9 %reduce-scatter.13.cloned.1.call-start = ((), (), s32[]{:S(2)}) async-start(), calls=%async_computation.11 | async-start | bytes 2359296 | tf_op jit(solution)/shard_map/reduce_scatter | solution.py:95
  410.0 205.1 %reduce-scatter.15.cloned.1.call-start = ((), (), s32[]{:S(2)}) async-start(), calls=%async_computation.12 | async-start | bytes 2359296 | tf_op jit(solution)/shard_map/reduce_scatter | solution.py:85
  484.7 7.7 collective-permute-start.14
  507.7 7.9 collective-permute-start.17
  515.6 9.0 %collective-permute-start.18 = (bf16[128,512]{1,0:T(8,128)(2,1)S(1)}, bf16[128,512]{1,0:T(8,128)(2,1)S(1)}, u32[]{:S(2)}, u32[]{:S(2)}) collective-permute-start(bf16[128,512]{1,0:T(8,128)(2,1)S(1)} %collective-permute-done.17), channel_id=1, source_target_pairs={{0,1},{1,2},{2,3},{3,4},{4,5},{5,6},{6,7},{7,0},{8,9},{9,10},{10,1... | collective-permute-start | bytes 393224 | tf_op jit(solution)/shard_map/ppermute | solution.py:107
  524.7 8.2 %collective-permute-start.19 = (bf16[128,512]{1,0:T(8,128)(2,1)S(1)}, bf16[128,512]{1,0:T(8,128)(2,1)S(1)}, u32[]{:S(2)}, u32[]{:S(2)}) collective-permute-start(bf16[128,512]{1,0:T(8,128)(2,1)S(1)} %collective-permute-done.18), channel_id=1, source_target_pairs={{0,1},{1,2},{2,3},{3,4},{4,5},{5,6},{6,7},{7,0},{8,9},{9,10},{10,1... | collective-permute-start | bytes 393224 | tf_op jit(solution)/shard_map/ppermute | solution.py:107
  549.4 106.8 %all-gather.8.cloned.1.call-start = ((), (), s32[]{:S(2)}) async-start(), calls=%async_computation.13 | async-start | bytes 1179648 | tf_op jit(solution)/shard_map/all_gather | solution.py:87
  616.8 119.9 %reduce-scatter.17.cloned.1.call-start = ((), (), s32[]{:S(2)}) async-start(), calls=%async_computation.14 | async-start | bytes 2359296 | tf_op jit(solution)/shard_map/reduce_scatter | solution.py:95
  744.2 7.7 collective-permute-start.23
  767.2 7.9 collective-permute-start.26
  775.2 9.1 %collective-permute-start.27 = (bf16[128,512]{1,0:T(8,128)(2,1)S(1)}, bf16[128,512]{1,0:T(8,128)(2,1)S(1)}, u32[]{:S(2)}, u32[]{:S(2)}) collective-permute-start(bf16[128,512]{1,0:T(8,128)(2,1)S(1)} %collective-permute-done.26), channel_id=1, source_target_pairs={{0,1},{1,2},{2,3},{3,4},{4,5},{5,6},{6,7},{7,0},{8,9},{9,10},{10,1... | collective-permute-start | bytes 393224 | tf_op jit(solution)/shard_map/ppermute | solution.py:107
  784.2 8.2 %collective-permute-start.28 = (bf16[128,512]{1,0:T(8,128)(2,1)S(1)}, bf16[128,512]{1,0:T(8,128)(2,1)S(1)}, u32[]{:S(2)}, u32[]{:S(2)}) collective-permute-start(bf16[128,512]{1,0:T(8,128)(2,1)S(1)} %collective-permute-done.27), channel_id=1, source_target_pairs={{0,1},{1,2},{2,3},{3,4},{4,5},{5,6},{6,7},{7,0},{8,9},{9,10},{10,1... | collective-permute-start | bytes 393224 | tf_op jit(solution)/shard_map/ppermute | solution.py:107
  (29 other events, 417.9 us)
Sparse Core Ops, SparseCore 0:
  28.5 69.3 reduce-scatter.6
  100.5 38.4 all-gather.3
  151.5 66.9 reduce-scatter.8
  291.0 65.5 reduce-scatter.10
  359.1 38.4 all-gather.5
  410.1 67.0 reduce-scatter.12
  549.5 65.5 reduce-scatter.14
  617.8 38.4 all-gather.7
  668.8 67.8 reduce-scatter.16
